TPU v7x, 32 devices: a whole 2x2x4 slice. The times are simulated.
32 devices in a mesh: row: 4 (over x, core), col: 4 (over z), depth: 2 (over y).
Axes of the slice: x: 2, y: 2, z: 4, core: 2. Of those that a mesh axis runs over, the one named last changes fastest.
Arguments:
- tokens: bfloat16 [512, 4096], P(('col', 'depth'), 'row'), may hold values from -6 to 6
- w_gate: bfloat16 [4096, 14336], P('row', 'col'), may hold values from -0.09375 to 0.09375
- w_up: bfloat16 [4096, 14336], P('row', 'col'), may hold values from -0.09375 to 0.09375
- w_down: bfloat16 [14336, 4096], P('col', 'row'), may hold values from -0.046875 to 0.046875
- cotangent: bfloat16 [512, 4096], P(('col', 'depth'), 'row'), may hold values from -0.25 to 0.25
Outputs:
- mixed: bfloat16 [512, 4096], P(('col', 'depth'), 'row')
- grad_gate: bfloat16 [4096, 14336], P(('row', 'depth'), 'col')
- grad_up: bfloat16 [4096, 14336], P(('row', 'depth'), 'col')
- grad_down: bfloat16 [14336, 4096], P(('col', 'depth'), 'row')
All inputs are finite; a program needn't handle non-finite values.
Results may differ from a plain program's by a relative error of at most 0.025.
Values may be sent and summed in bfloat16 or wider, within the bound.
A program may use at most 128 MiB of HBM per device.

v0:
```python
import jax
import jax.numpy as jnp
from jax import lax
from jax.sharding import PartitionSpec as P

COLS_CONTRACT = (((1,), (1,)), ((), ()))
ROWS_CONTRACT = (((0,), (0,)), ((), ()))


def gate_grads(hidden_grad, gate_sum, up_sum):
    sigmoid_gate = jax.nn.sigmoid(gate_sum)
    d_gate = (hidden_grad * up_sum * sigmoid_gate * (1.0 + gate_sum * (1.0 - sigmoid_gate))).astype(
        jnp.bfloat16
    )
    d_up = (hidden_grad * gate_sum * sigmoid_gate).astype(jnp.bfloat16)
    return (d_gate, d_up)


def per_device(tokens, w_gate, w_up, w_down, cotangent):
    hid_width = w_gate.shape[1]
    token_rows = lax.all_gather(tokens, "col", axis=0, tiled=True)
    row_piece = token_rows
    joined = lax.psum_scatter(
        jnp.concatenate(
            [
                jnp.dot(row_piece, w_gate, preferred_element_type=jnp.float32),
                jnp.dot(row_piece, w_up, preferred_element_type=jnp.float32),
            ],
            axis=1,
        ).astype(jnp.bfloat16),
        "row",
        scatter_dimension=0,
        tiled=True,
    ).astype(jnp.float32)
    gate_sum = joined[:, :hid_width]
    up_sum = joined[:, hid_width:]
    hidden = (jax.nn.silu(gate_sum) * up_sum).astype(jnp.bfloat16)
    hidden_rows = lax.all_gather(hidden, "row", axis=0, tiled=True)
    row_piece = hidden_rows
    mixed = lax.psum_scatter(
        jnp.dot(row_piece, w_down, preferred_element_type=jnp.float32).astype(jnp.bfloat16),
        "col",
        scatter_dimension=0,
        tiled=True,
    )
    cot_rows = lax.all_gather(cotangent, "col", axis=0, tiled=True)
    row_piece = cot_rows
    hidden_grad = lax.psum_scatter(
        lax.dot_general(
            row_piece, w_down, COLS_CONTRACT, preferred_element_type=jnp.float32
        ).astype(jnp.bfloat16),
        "row",
        scatter_dimension=0,
        tiled=True,
    ).astype(jnp.float32)
    d_gate, d_up = gate_grads(hidden_grad, gate_sum, up_sum)
    d_gate_rows, d_up_rows = (
        lax.all_gather(d_gate, "row", axis=0, tiled=True),
        lax.all_gather(d_up, "row", axis=0, tiled=True),
    )
    down_term = lax.dot_general(
        hidden_rows, cot_rows, ROWS_CONTRACT, preferred_element_type=jnp.float32
    )
    grad_down = lax.psum_scatter(
        down_term.astype(jnp.bfloat16), "depth", scatter_dimension=0, tiled=True
    )
    layer_tokens = lax.all_to_all(token_rows, "depth", split_axis=1, concat_axis=0, tiled=True)
    block_rows = token_rows.shape[0]
    empty_grad = jnp.zeros((layer_tokens.shape[1], d_gate_rows.shape[1]), jnp.float32)
    first_row = jnp.int32(0)
    gate_total = empty_grad
    up_total = empty_grad
    gate_piece = lax.all_gather(d_gate_rows, "depth", axis=0, tiled=True)
    up_piece = lax.all_gather(d_up_rows, "depth", axis=0, tiled=True)
    for sub_index in range(gate_piece.shape[0] // block_rows):
        gate_block = gate_piece[sub_index * block_rows : (sub_index + 1) * block_rows]
        up_block = up_piece[sub_index * block_rows : (sub_index + 1) * block_rows]
        offset = first_row + sub_index * block_rows
        tok_block = lax.dynamic_slice_in_dim(layer_tokens, offset, block_rows, 0)
        gate_part = lax.optimization_barrier(
            lax.dot_general(
                tok_block, gate_block, ROWS_CONTRACT, preferred_element_type=jnp.float32
            ).astype(jnp.bfloat16)
        )
        up_part = lax.optimization_barrier(
            lax.dot_general(
                tok_block, up_block, ROWS_CONTRACT, preferred_element_type=jnp.float32
            ).astype(jnp.bfloat16)
        )
        gate_total = gate_total + gate_part.astype(jnp.float32)
        up_total = up_total + up_part.astype(jnp.float32)
    return (mixed, gate_total.astype(jnp.bfloat16), up_total.astype(jnp.bfloat16), grad_down)


def solution(mesh):
    placed = (
        P(("col", "depth"), "row"),
        P("row", "col"),
        P("row", "col"),
        P("col", "row"),
        P(("col", "depth"), "row"),
    )
    return jax.shard_map(
        per_device,
        mesh=mesh,
        in_specs=placed,
        out_specs=(
            P(("col", "depth"), "row"),
            P(("row", "depth"), "col"),
            P(("row", "depth"), "col"),
            P(("col", "depth"), "row"),
        ),
        check_vma=False,
    )
```

profile of v0, /device:TPU:0, one launch (start us, length us, event | category | flops | bytes accessed | tf_op | source)
XLA Modules:
  0.0 411.8 jit_solution(894660631228663583)
XLA Ops:
  7.2 17.7 %all_gather.21 = bf16[256,1024]{1,0:T(8,128)(2,1)S(1)} all-gather(bf16[64,1024]{1,0:T(8,128)(2,1)} %param.5), channel_id=1, replica_groups=mesh['row'=4,'col'=4,'depth'=2] {'col'}, dimensions={0}, use_global_device_ids=true | all-gather | bytes 655360 | tf_op jit(solution)/shard_map/all_gather | solution.py:21
  24.9 5.3 %convolution_convert_fusion.6 = bf16[256,3584]{1,0:T(8,128)(2,1)S(1)} fusion(bf16[256,1024]{1,0:T(8,128)(2,1)S(1)} %all_gather.21, bf16[1024,3584]{1,0:T(8,128)(2,1)} %param.7), kind=kOutput, calls=%fused_computation.12 | convolution fusion | flops 1879965696 | bytes 9699328 | tf_op jit(solution)/shard_map/dot_general | solution.py:27
  30.3 2.1 convolution_convert_fusion.7
  32.4 2.3 pad_maximum_fusion
  34.7 0.8 copy-done.3
  35.5 16.2 %all_gather.23 = bf16[256,1024]{1,0:T(8,128)(2,1)S(1)} all-gather(bf16[64,1024]{1,0:T(8,128)(2,1)S(1)} %copy-done.3), channel_id=1, replica_groups=mesh['row'=4,'col'=4,'depth'=2] {'col'}, dimensions={0}, use_global_device_ids=true | all-gather | bytes 655360 | tf_op jit(solution)/shard_map/all_gather | solution.py:46
  51.8 6.5 %convolution_convert_fusion.5 = bf16[256,3584]{1,0:T(8,128)(2,1)} fusion(bf16[256,1024]{1,0:T(8,128)(2,1)S(1)} %all_gather.23, bf16[3584,1024]{1,0:T(8,128)(2,1)} %param.8), kind=kOutput, calls=%fused_computation.11 | convolution fusion | flops 1879965696 | bytes 9699328 | tf_op jit(solution)/shard_map/dot_general | solution.py:49
  58.3 19.4 %reduce-scatter.5.cloned.1.call-done = bf16[64,7168]{1,0:T(8,128)(2,1)} async-done(((bf16[256,7168]{1,0:T(8,128)(2,1)}), bf16[64,7168]{1,0:T(8,128)(2,1)}) %reduce-scatter.5.cloned.1.call-update) | async-done | bytes 917520 | tf_op jit(solution)/shard_map/reduce_scatter | solution.py:23
  77.8 1.3 convert_element_type.67
  79.1 31.5 %reduce-scatter.9.cloned.1.call-done = bf16[64,3584]{1,0:T(8,128)(2,1)} async-done(((bf16[256,3584]{1,0:T(8,128)(2,1)}), bf16[64,3584]{1,0:T(8,128)(2,1)}) %reduce-scatter.9.cloned.1.call-update) | async-done | bytes 458768 | tf_op jit(solution)/shard_map/reduce_scatter | solution.py:48
  110.5 2.5 fusion.12
  113.1 0.5 all-gather.12.cloned.1.call-update
  113.7 0.5 all-gather.6.cloned.1.call-update
  114.3 20.0 %all-gather.8.cloned.1.call-done = bf16[256,3584]{1,0:T(8,128)(2,1)} async-done(((bf16[64,3584]{1,0:T(8,128)(2,1)}), bf16[256,3584]{1,0:T(8,128)(2,1)}) %all-gather.8.cloned.1.call-update) | async-done | bytes 1835024 | tf_op jit(solution)/shard_map/all_gather | solution.py:58
  134.4 23.1 %all-gather.12.cloned.1.call-done = bf16[256,3584]{1,0:T(8,128)(2,1)} async-done(((bf16[64,3584]{1,0:T(8,128)(2,1)}), bf16[256,3584]{1,0:T(8,128)(2,1)}) %all-gather.12.cloned.1.call-update) | async-done | bytes 1835024 | tf_op jit(solution)/shard_map/all_gather | solution.py:59
  157.5 23.0 %all-gather.6.cloned.1.call-done = bf16[256,3584]{1,0:T(8,128)(2,1)} async-done(((bf16[64,3584]{1,0:T(8,128)(2,1)}), bf16[256,3584]{1,0:T(8,128)(2,1)}) %all-gather.6.cloned.1.call-update) | async-done | bytes 1835024 | tf_op jit(solution)/shard_map/all_gather | solution.py:38
  180.6 6.6 %convolution_convert_fusion.8 = bf16[256,1024]{1,0:T(8,128)(2,1)} fusion(bf16[256,3584]{1,0:T(8,128)(2,1)} %all-gather.6.cloned.1.call-done, bf16[3584,1024]{1,0:T(8,128)(2,1)} %param.8), kind=kOutput, calls=%fused_computation.19 | convolution fusion | flops 1879310336 | bytes 9699328 | tf_op jit(solution)/shard_map/dot_general | solution.py:41
  187.3 5.3 %convolution_convert_fusion = bf16[3584,1024]{1,0:T(8,128)(2,1)} fusion(bf16[256,3584]{1,0:T(8,128)(2,1)S(1)} %copy-done.2, bf16[256,1024]{1,0:T(8,128)(2,1)S(1)} %all_gather.23), kind=kOutput, calls=%fused_computation | convolution fusion | flops 1882718208 | bytes 9699328 | tf_op jit(solution)/shard_map/dot_general | solution.py:61
  192.6 0.2 copy.18
  192.9 17.3 %all_to_all.16 = bf16[256,2,512]{0,2,1:T(8,128)(2,1)S(1)} all-to-all(bf16[256,2,512]{0,2,1:T(8,128)(2,1)S(1)} %bitcast.36), channel_id=1, replica_groups=mesh['row'=4,'col'=4,'depth'=2] {'depth'}, dimensions={1} | all-to-all | bytes 1048576 | tf_op jit(solution)/shard_map/all_to_all | solution.py:67
  210.2 28.3 %all-gather.10.cloned.1.call-done = bf16[512,3584]{1,0:T(8,128)(2,1)} async-done(((bf16[256,3584]{1,0:T(8,128)(2,1)}), bf16[512,3584]{1,0:T(8,128)(2,1)}) %all-gather.10.cloned.1.call-update) | async-done | bytes 3670032 | tf_op jit(solution)/shard_map/all_gather | solution.py:73
  238.4 2.8 fusion
  241.3 1.2 fusion.1
  242.5 2.9 add_convert_fusion.1
  245.3 6.1 %copy.21 = bf16[512,3584]{1,0:T(8,128)(2,1)} copy(bf16[512,3584]{0,1:T(8,128)(2,1)} %add_convert_fusion.1) | data formatting | bytes 7340032
  251.5 39.4 %all-gather.14.cloned.1.call-done = bf16[512,3584]{1,0:T(8,128)(2,1)} async-done(((bf16[256,3584]{1,0:T(8,128)(2,1)}), bf16[512,3584]{1,0:T(8,128)(2,1)}) %all-gather.14.cloned.1.call-update) | async-done | bytes 3670032 | tf_op jit(solution)/shard_map/all_gather | solution.py:74
  290.8 2.8 fusion.2
  293.7 1.2 fusion.3
  294.9 3.0 add_convert_fusion
  297.8 5.9 %copy.22 = bf16[512,3584]{1,0:T(8,128)(2,1)} copy(bf16[512,3584]{0,1:T(8,128)(2,1)} %add_convert_fusion) | data formatting | bytes 7340032
  303.7 11.8 %reduce-scatter.7.cloned.1.call-done = bf16[64,1024]{1,0:T(8,128)(2,1)} async-done(((bf16[256,1024]{1,0:T(8,128)(2,1)}), bf16[64,1024]{1,0:T(8,128)(2,1)}) %reduce-scatter.7.cloned.1.call-update) | async-done | bytes 131088 | tf_op jit(solution)/shard_map/reduce_scatter | solution.py:40
  315.5 89.7 %reduce-scatter.11.cloned.1.call-done = bf16[1792,1024]{1,0:T(8,128)(2,1)} async-done(((bf16[3584,1024]{1,0:T(8,128)(2,1)}), bf16[1792,1024]{1,0:T(8,128)(2,1)}) %reduce-scatter.11.cloned.1.call-update) | async-done | bytes 3670032 | tf_op jit(solution)/shard_map/reduce_scatter | solution.py:64
  (28 shorter events, 0.5 us)
Async XLA Ops:
  7.2 70.6 %reduce-scatter.5.cloned.1.call-start = ((), (), s32[]{:S(2)}) async-start(), calls=%async_computation.5 | async-start | bytes 4587520 | tf_op jit(solution)/shard_map/reduce_scatter | solution.py:23
  7.2 23.0 %slice-start = ((s8[7340032]{0:T(1024)(128)(4,1)}), s8[4194304]{0:T(1024)(128)(4,1)S(1)}, s32[]{:S(2)}) async-start(s8[7340032]{0:T(1024)(128)(4,1)} %bitcast.37), calls=%async_computation.14 | async-start | bytes 8388608
  24.9 5.3 %slice-start.1 = ((s8[7340032]{0:T(1024)(128)(4,1)}), s8[3145728]{0:T(1024)(128)(4,1)S(1)}, s32[]{:S(2)}) async-start(s8[7340032]{0:T(1024)(128)(4,1)} %bitcast.37), calls=%async_computation.15 | async-start | bytes 6291456
  34.6 0.9 copy-start.3
  34.6 75.9 %reduce-scatter.9.cloned.1.call-start = ((), (), s32[]{:S(2)}) async-start(), calls=%async_computation.8 | async-start | bytes 2293760 | tf_op jit(solution)/shard_map/reduce_scatter | solution.py:48
  58.3 76.1 %all-gather.8.cloned.1.call-start = ((), (), s32[]{:S(2)}) async-start(), calls=%async_computation.9 | async-start | bytes 2293760 | tf_op jit(solution)/shard_map/all_gather | solution.py:58
  113.1 44.4 %all-gather.12.cloned.1.call-start = ((), (), s32[]{:S(2)}) async-start(), calls=%async_computation.11 | async-start | bytes 2293760 | tf_op jit(solution)/shard_map/all_gather | solution.py:59
  113.7 66.9 %all-gather.6.cloned.1.call-start = ((), (), s32[]{:S(2)}) async-start(), calls=%async_computation.6 | async-start | bytes 2293760 | tf_op jit(solution)/shard_map/all_gather | solution.py:38
  114.3 124.2 %all-gather.10.cloned.1.call-start = ((), (), s32[]{:S(2)}) async-start(), calls=%async_computation.10 | async-start | bytes 5505024 | tf_op jit(solution)/shard_map/all_gather | solution.py:73
  134.4 156.5 %all-gather.14.cloned.1.call-start = ((), (), s32[]{:S(2)}) async-start(), calls=%async_computation.12 | async-start | bytes 5505024 | tf_op jit(solution)/shard_map/all_gather | solution.py:74
  157.5 158.1 %reduce-scatter.7.cloned.1.call-start = ((), (), s32[]{:S(2)}) async-start(), calls=%async_computation.7 | async-start | bytes 655360 | tf_op jit(solution)/shard_map/reduce_scatter | solution.py:40
  180.6 6.7 %copy-start.2 = (bf16[256,3584]{1,0:T(8,128)(2,1)S(1)}, bf16[256,3584]{1,0:T(8,128)(2,1)}, u32[]{:S(2)}) copy-start(bf16[256,3584]{1,0:T(8,128)(2,1)} %all-gather.6.cloned.1.call-done) | copy-start | bytes 5505028
  187.2 218.0 %reduce-scatter.11.cloned.1.call-start = ((), (), s32[]{:S(2)}) async-start(), calls=%async_computation.13 | async-start | bytes 11010048 | tf_op jit(solution)/shard_map/reduce_scatter | solution.py:64
  238.4 2.8 copy-start
  290.8 2.8 copy-start.1
Sparse Core Ops, SparseCore 0:
  34.8 42.9 reduce-scatter.4
  80.9 29.6 reduce-scatter.8
  113.2 21.0 all-gather.7
  136.3 21.0 all-gather.11
  159.4 21.0 all-gather.5
  182.0 56.4 all-gather.9
  240.0 50.8 all-gather.13
  293.7 21.8 reduce-scatter.6
  318.4 86.7 reduce-scatter.10
where the time goes:
time: 412 us
  waiting for transfers between devices  287 us (70%)
  blocking collectives  51.3 us (12%)
  matrix products  33.8 us (8%)
  between operations  14 us (3%)
  local copies, waits for them, and re-layouts  13.1 us (3%)
  other arithmetic  11.9 us (3%)
    reduce_scatter x1, waiting for transfers between devices, per_device(): lax.psum_scatter(down_term.astype(jnp.bfloat16), 'depth', scatter_dimensi...  89.7 us
    all_gather x1, waiting for transfers between devices, per_device(): up_piece = lax.all_gather(d_up_rows, 'depth', axis=0, tiled=True)  39.4 us
    reduce_scatter x1, waiting for transfers between devices, per_device(): lax.psum_scatter(lax.dot_general(row_piece, w_down, COLS_CONTRACT, prefer...  31.5 us
    all_gather x1, waiting for transfers between devices, per_device(): gate_piece = lax.all_gather(d_gate_rows, 'depth', axis=0, tiled=True)  28.3 us
    all_gather x1, waiting for transfers between devices, per_device(): lax.all_gather(d_up, 'row', axis=0, tiled=True)  23.1 us
    all_gather x1, waiting for transfers between devices, per_device(): hidden_rows = lax.all_gather(hidden, 'row', axis=0, tiled=True)  23 us
    all_gather x1, waiting for transfers between devices, per_device(): lax.all_gather(d_gate, 'row', axis=0, tiled=True)  20 us
    reduce_scatter x1, waiting for transfers between devices, per_device(): lax.psum_scatter(jnp.concatenate([jnp.dot(row_piece, w_gate, preferred_el...  19.4 us
  transfers between devices with their start and end apart: 9, of which 9 were waited for; matrix products, arithmetic and copies ran while one was open for 11% of the time, Pallas kernels for 0%

commit v1 on v0

--- a/solution.py
+++ b/solution.py
@@ -35,7 +35,12 @@
     gate_sum = joined[:, :hid_width]
     up_sum = joined[:, hid_width:]
     hidden = (jax.nn.silu(gate_sum) * up_sum).astype(jnp.bfloat16)
-    hidden_rows = lax.all_gather(hidden, "row", axis=0, tiled=True)
+    ring = [hidden]
+    for hop in range(3):
+        ring.append(lax.ppermute(ring[-1], "row", [(dev, (dev + 1) % 4) for dev in range(4)]))
+    hidden_rows = jnp.roll(
+        jnp.concatenate(ring[::-1], axis=0), (lax.axis_index("row") + 1) * ring[0].shape[0], axis=0
+    )
     row_piece = hidden_rows
     mixed = lax.psum_scatter(
         jnp.dot(row_piece, w_down, preferred_element_type=jnp.float32).astype(jnp.bfloat16),

time: 412 us -> 393 us (0.954)
  waiting for transfers between devices: 287 us -> 261 us
  local copies, waits for them, and re-layouts: 13.1 us -> 19.5 us
    ppermute x0 -> x3, waiting for transfers between devices: none -> 31.7 us  [per_device(): lax.ppermute(ring[-1], 'row', [(dev, (dev + 1) % 4) for dev in range(4)])]
    all_gather x1, waiting for transfers between devices: 23.1 us -> 0.01 us  [per_device(): lax.all_gather(d_up, 'row', axis=0, tiled=True)]
    all_gather x1 -> x0, waiting for transfers between devices: 23 us -> none  [per_device(): hidden_rows = lax.all_gather(hidden, 'row', axis=0, tiled=True)]
    all_gather x1, waiting for transfers between devices: 28.3 us -> 16.1 us  [per_device(): gate_piece = lax.all_gather(d_gate_rows, 'depth', axis=0, tiled=True)]
    unnamed x14 -> x19, local copies, waits for them, and re-layouts: 12.9 us -> 18.5 us
  transfers between devices with their start and end apart: 9 -> 11, of which waited for: 9 -> 10; matrix products, arithmetic and copies ran while one was open for 11% -> 14% of each run, Pallas kernels for 0% -> 0%
where the time goes in v1:
time: 393 us
  waiting for transfers between devices  261 us (66%)
  blocking collectives  50.7 us (13%)
  matrix products  35.4 us (9%)
  local copies, waits for them, and re-layouts  19.5 us (5%)
  between operations  14.2 us (4%)
  other arithmetic  11.8 us (3%)
    reduce_scatter x1, waiting for transfers between devices, per_device(): lax.psum_scatter(down_term.astype(jnp.bfloat16), 'depth', scatter_dimensi...  89.7 us
    all_gather x1, waiting for transfers between devices, per_device(): up_piece = lax.all_gather(d_up_rows, 'depth', axis=0, tiled=True)  39.2 us
    ppermute x3, waiting for transfers between devices, per_device(): lax.ppermute(ring[-1], 'row', [(dev, (dev + 1) % 4) for dev in range(4)])  31.7 us
    reduce_scatter x1, waiting for transfers between devices, per_device(): lax.psum_scatter(lax.dot_general(row_piece, w_down, COLS_CONTRACT, prefer...  31.5 us
    all_gather x1, waiting for transfers between devices, per_device(): lax.all_gather(d_gate, 'row', axis=0, tiled=True)  20.6 us
    reduce_scatter x1, waiting for transfers between devices, per_device(): lax.psum_scatter(jnp.concatenate([jnp.dot(row_piece, w_gate, preferred_el...  19.4 us
    unnamed x19, local copies, waits for them, and re-layouts  18.5 us
    all_gather x1, blocking collectives, per_device(): token_rows = lax.all_gather(tokens, 'col', axis=0, tiled=True)  17.7 us
  transfers between devices with their start and end apart: 11, of which 10 were waited for; matrix products, arithmetic and copies ran while one was open for 14% of the time, Pallas kernels for 0%

profile of v1, /device:TPU:0, one launch (start us, length us, event | category | flops | bytes accessed | tf_op | source)
XLA Modules:
  0.0 392.9 jit_solution(6578446263304724114)
XLA Ops:
  7.2 17.7 %all_gather.18 = bf16[256,1024]{1,0:T(8,128)(2,1)S(1)} all-gather(bf16[64,1024]{1,0:T(8,128)(2,1)} %param.5), channel_id=1, replica_groups=mesh['row'=4,'col'=4,'depth'=2] {'col'}, dimensions={0}, use_global_device_ids=true | all-gather | bytes 655360 | tf_op jit(solution)/shard_map/all_gather | solution.py:21
  24.9 5.3 %convolution_convert_fusion.6 = bf16[256,3584]{1,0:T(8,128)(2,1)S(1)} fusion(bf16[256,1024]{1,0:T(8,128)(2,1)S(1)} %all_gather.18, bf16[1024,3584]{1,0:T(8,128)(2,1)} %param.7), kind=kOutput, calls=%fused_computation.12 | convolution fusion | flops 1879965696 | bytes 9699328 | tf_op jit(solution)/shard_map/dot_general | solution.py:27
  30.3 2.1 convolution_convert_fusion.7
  32.4 2.3 pad_maximum_fusion
  34.7 0.8 copy-done.2
  35.5 16.2 %all_gather.19 = bf16[256,1024]{1,0:T(8,128)(2,1)S(1)} all-gather(bf16[64,1024]{1,0:T(8,128)(2,1)S(1)} %copy-done.2), channel_id=1, replica_groups=mesh['row'=4,'col'=4,'depth'=2] {'col'}, dimensions={0}, use_global_device_ids=true | all-gather | bytes 655360 | tf_op jit(solution)/shard_map/all_gather | solution.py:51
  51.8 6.5 %convolution_convert_fusion.5 = bf16[256,3584]{1,0:T(8,128)(2,1)} fusion(bf16[256,1024]{1,0:T(8,128)(2,1)S(1)} %all_gather.19, bf16[3584,1024]{1,0:T(8,128)(2,1)} %param.8), kind=kOutput, calls=%fused_computation.11 | convolution fusion | flops 1879965696 | bytes 9699328 | tf_op jit(solution)/shard_map/dot_general | solution.py:54
  58.3 19.4 %reduce-scatter.5.cloned.1.call-done = bf16[64,7168]{1,0:T(8,128)(2,1)} async-done(((bf16[256,7168]{1,0:T(8,128)(2,1)}), bf16[64,7168]{1,0:T(8,128)(2,1)}) %reduce-scatter.5.cloned.1.call-update) | async-done | bytes 917520 | tf_op jit(solution)/shard_map/reduce_scatter | solution.py:23
  77.8 1.3 convert_element_type.67
  79.1 31.5 %reduce-scatter.9.cloned.1.call-done = bf16[64,3584]{1,0:T(8,128)(2,1)} async-done(((bf16[256,3584]{1,0:T(8,128)(2,1)}), bf16[64,3584]{1,0:T(8,128)(2,1)}) %reduce-scatter.9.cloned.1.call-update) | async-done | bytes 458768 | tf_op jit(solution)/shard_map/reduce_scatter | solution.py:53
  110.5 2.4 fusion.18
  113.6 20.6 %all-gather.5.cloned.1.call-done = bf16[256,3584]{1,0:T(8,128)(2,1)} async-done(((bf16[64,3584]{1,0:T(8,128)(2,1)}), bf16[256,3584]{1,0:T(8,128)(2,1)}) %all-gather.5.cloned.1.call-update) | async-done | bytes 1835024 | tf_op jit(solution)/shard_map/all_gather | solution.py:63
  134.6 7.7 %collective-permute-done = bf16[64,3584]{1,0:T(8,128)(2,1)S(1)} collective-permute-done((bf16[64,3584]{1,0:T(8,128)(2,1)S(1)}, bf16[64,3584]{1,0:T(8,128)(2,1)S(1)}, u32[]{:S(2)}, u32[]{:S(2)}) %collective-permute-start) | collective-permute-done | bytes 458784 | tf_op jit(solution)/shard_map/ppermute | solution.py:40
  142.3 16.1 %collective-permute-done.1 = bf16[64,3584]{1,0:T(8,128)(2,1)S(1)} collective-permute-done((bf16[64,3584]{1,0:T(8,128)(2,1)S(1)}, bf16[64,3584]{1,0:T(8,128)(2,1)S(1)}, u32[]{:S(2)}, u32[]{:S(2)}) %collective-permute-start.1) | collective-permute-done | bytes 458784 | tf_op jit(solution)/shard_map/ppermute | solution.py:40
  158.4 7.9 %collective-permute-done.2 = bf16[64,3584]{1,0:T(8,128)(2,1)S(1)} collective-permute-done((bf16[64,3584]{1,0:T(8,128)(2,1)S(1)}, bf16[64,3584]{1,0:T(8,128)(2,1)S(1)}, u32[]{:S(2)}, u32[]{:S(2)}) %collective-permute-start.2) | collective-permute-done | bytes 458784 | tf_op jit(solution)/shard_map/ppermute | solution.py:40
  166.3 0.8 constant_dynamic-update-slice_fusion.7
  167.1 0.8 constant_dynamic-update-slice_fusion.6
  172.7 7.0 %fusion.11 = bf16[256,1024]{1,0:T(8,128)(2,1)} fusion(bf16[3584,1024]{1,0:T(8,128)(2,1)} %param.8, bf16[512,3584]{1,0:T(8,128)(2,1)} %constant_dynamic-update-slice_fusion, s32[]{:T(128)S(6)} %select_n.14), kind=kOutput, calls=%fused_computation.22 | convolution fusion | flops 1879310336 | bytes 9699332 | tf_op jit(solution)/shard_map/dot_general | solution.py:46
  179.8 6.6 %convolution_convert_fusion = bf16[3584,1024]{1,0:T(8,128)(2,1)} fusion(bf16[256,1024]{1,0:T(8,128)(2,1)S(1)} %all_gather.19, bf16[512,3584]{1,0:T(8,128)(2,1)} %constant_dynamic-update-slice_fusion, s32[]{:T(128)S(6)} %select_n.14), kind=kOutput, calls=%fused_computation | convolution fusion | flops 1882718208 | bytes 9699332 | tf_op jit(solution)/shard_map/dot_general | solution.py:66
  186.6 16.8 %all_to_all.16 = bf16[256,2,512]{0,2,1:T(8,128)(2,1)S(1)} all-to-all(bf16[256,2,512]{0,2,1:T(8,128)(2,1)S(1)} %bitcast.34), channel_id=1, replica_groups=mesh['row'=4,'col'=4,'depth'=2] {'depth'}, dimensions={1} | all-to-all | bytes 1048576 | tf_op jit(solution)/shard_map/all_to_all | solution.py:72
  203.3 16.1 %all-gather.7.cloned.1.call-done = bf16[512,3584]{1,0:T(8,128)(2,1)} async-done(((bf16[256,3584]{1,0:T(8,128)(2,1)}), bf16[512,3584]{1,0:T(8,128)(2,1)}) %all-gather.7.cloned.1.call-update) | async-done | bytes 3670032 | tf_op jit(solution)/shard_map/all_gather | solution.py:78
  219.4 2.8 fusion
  222.2 1.2 fusion.1
  223.4 2.9 add_convert_fusion.1
  226.3 6.2 %copy.21 = bf16[512,3584]{1,0:T(8,128)(2,1)} copy(bf16[512,3584]{0,1:T(8,128)(2,1)} %add_convert_fusion.1) | data formatting | bytes 7340032
  232.4 39.2 %all-gather.11.cloned.1.call-done = bf16[512,3584]{1,0:T(8,128)(2,1)} async-done(((bf16[256,3584]{1,0:T(8,128)(2,1)}), bf16[512,3584]{1,0:T(8,128)(2,1)}) %all-gather.11.cloned.1.call-update) | async-done | bytes 3670032 | tf_op jit(solution)/shard_map/all_gather | solution.py:79
  271.6 2.8 fusion.2
  274.5 1.2 fusion.3
  275.7 3.0 add_convert_fusion
  278.6 5.9 %copy.22 = bf16[512,3584]{1,0:T(8,128)(2,1)} copy(bf16[512,3584]{0,1:T(8,128)(2,1)} %add_convert_fusion) | data formatting | bytes 7340032
  284.5 11.8 %reduce-scatter.7.cloned.1.call-done = bf16[64,1024]{1,0:T(8,128)(2,1)} async-done(((bf16[256,1024]{1,0:T(8,128)(2,1)}), bf16[64,1024]{1,0:T(8,128)(2,1)}) %reduce-scatter.7.cloned.1.call-update) | async-done | bytes 131088 | tf_op jit(solution)/shard_map/reduce_scatter | solution.py:45
  296.3 89.7 %reduce-scatter.11.cloned.1.call-done = bf16[1792,1024]{1,0:T(8,128)(2,1)} async-done(((bf16[3584,1024]{1,0:T(8,128)(2,1)}), bf16[1792,1024]{1,0:T(8,128)(2,1)}) %reduce-scatter.11.cloned.1.call-update) | async-done | bytes 3670032 | tf_op jit(solution)/shard_map/reduce_scatter | solution.py:69
  (37 shorter events, 6.2 us)
Async XLA Ops:
  7.2 70.6 %reduce-scatter.5.cloned.1.call-start = ((), (), s32[]{:S(2)}) async-start(), calls=%async_computation.5 | async-start | bytes 4587520 | tf_op jit(solution)/shard_map/reduce_scatter | solution.py:23
  7.2 23.0 %slice-start = ((s8[7340032]{0:T(1024)(128)(4,1)}), s8[4194304]{0:T(1024)(128)(4,1)S(1)}, s32[]{:S(2)}) async-start(s8[7340032]{0:T(1024)(128)(4,1)} %bitcast.35), calls=%async_computation.13 | async-start | bytes 8388608
  24.9 5.3 %slice-start.1 = ((s8[7340032]{0:T(1024)(128)(4,1)}), s8[3145728]{0:T(1024)(128)(4,1)S(1)}, s32[]{:S(2)}) async-start(s8[7340032]{0:T(1024)(128)(4,1)} %bitcast.35), calls=%async_computation.14 | async-start | bytes 6291456
  34.6 0.9 copy-start.2
  34.6 75.9 %reduce-scatter.9.cloned.1.call-start = ((), (), s32[]{:S(2)}) async-start(), calls=%async_computation.7 | async-start | bytes 2293760 | tf_op jit(solution)/shard_map/reduce_scatter | solution.py:53
  58.3 76.0 %all-gather.5.cloned.1.call-start = ((), (), s32[]{:S(2)}) async-start(), calls=%async_computation.8 | async-start | bytes 2293760 | tf_op jit(solution)/shard_map/all_gather | solution.py:63
  113.0 54.1 %all-gather.9.cloned.1.call-start = ((), (), s32[]{:S(2)}) async-start(), calls=%async_computation.10 | async-start | bytes 2293760 | tf_op jit(solution)/shard_map/all_gather | solution.py:64
  113.6 105.8 %all-gather.7.cloned.1.call-start = ((), (), s32[]{:S(2)}) async-start(), calls=%async_computation.9 | async-start | bytes 5505024 | tf_op jit(solution)/shard_map/all_gather | solution.py:78
  134.3 137.4 %all-gather.11.cloned.1.call-start = ((), (), s32[]{:S(2)}) async-start(), calls=%async_computation.11 | async-start | bytes 5505024 | tf_op jit(solution)/shard_map/all_gather | solution.py:79
  134.3 8.0 %collective-permute-start = (bf16[64,3584]{1,0:T(8,128)(2,1)S(1)}, bf16[64,3584]{1,0:T(8,128)(2,1)S(1)}, u32[]{:S(2)}, u32[]{:S(2)}) collective-permute-start(bf16[64,3584]{1,0:T(8,128)(2,1)S(1)} %get-tuple-element.22), channel_id=1, source_target_pairs={{0,8},{8,16},{16,24},{24,0},{1,9},{9,17},{17,25},{25,1},{2,10},{10... | collective-permute-start | bytes 1376264 | tf_op jit(solution)/shard_map/ppermute | solution.py:40
  142.3 16.1 %collective-permute-start.1 = (bf16[64,3584]{1,0:T(8,128)(2,1)S(1)}, bf16[64,3584]{1,0:T(8,128)(2,1)S(1)}, u32[]{:S(2)}, u32[]{:S(2)}) collective-permute-start(bf16[64,3584]{1,0:T(8,128)(2,1)S(1)} %collective-permute-done), channel_id=1, source_target_pairs={{0,8},{8,16},{16,24},{24,0},{1,9},{9,17},{17,25},{25,1},{2,10},{10... | collective-permute-start | bytes 1376264 | tf_op jit(solution)/shard_map/ppermute | solution.py:40
  158.4 7.9 %collective-permute-start.2 = (bf16[64,3584]{1,0:T(8,128)(2,1)S(1)}, bf16[64,3584]{1,0:T(8,128)(2,1)S(1)}, u32[]{:S(2)}, u32[]{:S(2)}) collective-permute-start(bf16[64,3584]{1,0:T(8,128)(2,1)S(1)} %collective-permute-done.1), channel_id=1, source_target_pairs={{0,8},{8,16},{16,24},{24,0},{1,9},{9,17},{17,25},{25,1},{2,10},{10... | collective-permute-start | bytes 1376264 | tf_op jit(solution)/shard_map/ppermute | solution.py:40
  167.1 129.3 %reduce-scatter.7.cloned.1.call-start = ((), (), s32[]{:S(2)}) async-start(), calls=%async_computation.6 | async-start | bytes 655360 | tf_op jit(solution)/shard_map/reduce_scatter | solution.py:45
  179.7 206.3 %reduce-scatter.11.cloned.1.call-start = ((), (), s32[]{:S(2)}) async-start(), calls=%async_computation.12 | async-start | bytes 11010048 | tf_op jit(solution)/shard_map/reduce_scatter | solution.py:69
  219.4 2.8 copy-start
  271.6 2.8 copy-start.1
Sparse Core Ops, SparseCore 0:
  34.8 42.9 reduce-scatter.4
  80.9 29.6 reduce-scatter.8
  113.1 21.0 all-gather.4
  136.2 25.2 all-gather.8
  162.9 56.4 all-gather.6
  220.8 50.8 all-gather.10
  274.5 21.8 reduce-scatter.6
  299.2 86.7 reduce-scatter.10
